TPU v7x, 32 devices: a whole 2x2x4 slice. The times are simulated.
32 devices in a mesh: dp: 4 (over z), ctx: 4 (over y, core), tp: 2 (over x).
Axes of the slice: x: 2, y: 2, z: 4, core: 2. Of those that a mesh axis runs over, the one named last changes fastest.
Arguments:
- queries: bfloat16 [4, 512, 4096], P('dp', 'ctx', 'tp'), may hold values from -8 to 8
- keys_text: bfloat16 [4, 512, 512], P('dp', 'ctx', 'tp'), may hold values from -8 to 8
- values_text: bfloat16 [4, 512, 512], P('dp', 'ctx', 'tp'), may hold values from -6 to 6
- patch_rows: bfloat16 [4, 4, 8, 2, 512], P('dp', 'ctx', None, None, 'tp'), may hold values from -6 to 6
- patch_owner: int32 [4, 4, 8, 1], P('dp', 'ctx'), may hold values from 0 to 3; in each aligned block of 8 rows (0 to 7, 8 to 15, ..., all dimensions but the last counted through in order) at most 4 rows name the same one
- patch_place: int32 [4, 4, 8], P('dp', 'ctx'), may hold values from 0 to 127
- value_head: bfloat16 [4096], P('tp'), may hold values from -0.75 to 0.75
Outputs:
- attention: bfloat16 [4, 512, 4096], P('dp', 'ctx', 'tp')
- value_out: float32 [4, 512], P('dp', 'ctx')
Inputs may be any that keep to these rules, and one draw needn't show every extreme that they name: `patch_owner`: among the rows of one vision shard at most 4 name the same sequence, and exactly 4 do in some shards. `patch_place`: rows that share an owner, a ctx index and a position are all added there.
All inputs are finite; a program needn't handle non-finite values.
Results may differ from a plain program's by a relative error of at most 0.0079.
Values may be sent and summed in bfloat16 or wider, within the bound.
A program may use at most 64 MiB of HBM per device.

v0:
```python
import jax
import jax.numpy as jnp
from jax import lax
from jax.sharding import PartitionSpec as P

HD = 128
CAP = 4


def attend_block(
    carried, query_split, query_place, block_keys, block_values, key_place, score_scale
):
    running_max, denominator, numerator = carried
    scores = (
        jnp.einsum("tgrd,sgd->tgrs", query_split, block_keys, preferred_element_type=jnp.float32)
        * score_scale
    )
    allowed = (key_place[None, :] <= query_place[:, None])[:, None, None, :]
    scores = jnp.where(allowed, scores, -1e30)
    new_max = jnp.maximum(running_max, jnp.max(scores, axis=-1))
    weights = jnp.where(allowed, jnp.exp(scores - new_max[..., None]), 0.0)
    shrink = jnp.exp(running_max - new_max)
    denominator = denominator * shrink + jnp.sum(weights, axis=-1)
    numerator = numerator * shrink[..., None] + jnp.einsum(
        "tgrs,sgd->tgrd",
        weights.astype(jnp.bfloat16),
        block_values,
        preferred_element_type=jnp.float32,
    )
    return (new_max, denominator, numerator)


def unchanged(carried):
    return carried


def body(queries, keys_text, values_text, patch_rows, patch_owner, patch_place, value_head):
    token_count = queries.shape[1]
    kv_width = keys_text.shape[2]
    groups = kv_width // HD
    head_count = queries.shape[2] // HD
    group_size = head_count // groups
    score_scale = HD ** (-0.5)
    dp_count = lax.axis_size("dp")
    slot_count = dp_count * CAP
    owner_seq = patch_owner[0, 0, :, 0]
    places = patch_place[0, 0]
    owner_hits = (owner_seq[:, None] == jnp.arange(dp_count, dtype=jnp.int32)[None, :]).astype(
        jnp.int32
    )
    before = jnp.cumsum(owner_hits, axis=0) - owner_hits
    slot_rank = jnp.sum(before * owner_hits, axis=1)
    target = owner_seq * CAP + slot_rank
    select = (jnp.arange(slot_count, dtype=jnp.int32)[:, None] == target[None, :]).astype(jnp.int32)
    row_data = patch_rows[0, 0].reshape(places.shape[0], 2 * kv_width)
    packed = jnp.dot(
        select.astype(jnp.bfloat16), row_data, preferred_element_type=jnp.float32
    ).astype(jnp.bfloat16)
    filled = jnp.sum(select, axis=1)
    slot_place = jnp.sum(select * places[None, :], axis=1) + (1 - filled) * token_count
    packed = packed.reshape(slot_count, 2, kv_width)
    arrived, arrived_place = (
        lax.all_to_all(packed, "dp", split_axis=0, concat_axis=0, tiled=True),
        lax.all_to_all(slot_place, "dp", split_axis=0, concat_axis=0, tiled=True),
    )
    landing = (jnp.arange(token_count, dtype=jnp.int32)[:, None] == arrived_place[None, :]).astype(
        jnp.bfloat16
    )
    arrivals = jnp.dot(
        landing, arrived.reshape(slot_count, 2 * kv_width), preferred_element_type=jnp.float32
    )
    merged_keys = (keys_text[0].astype(jnp.float32) + arrivals[:, :kv_width]).astype(jnp.bfloat16)
    merged_values = (values_text[0].astype(jnp.float32) + arrivals[:, kv_width:]).astype(
        jnp.bfloat16
    )
    query_split = queries[0].reshape(token_count, groups, group_size, HD)
    first_row = lax.axis_index("ctx") * token_count
    query_place = first_row + jnp.arange(token_count, dtype=jnp.int32)
    initial = (
        jnp.full((token_count, groups, group_size), -1e30, jnp.float32),
        jnp.zeros((token_count, groups, group_size), jnp.float32),
        jnp.zeros((token_count, groups, group_size, HD), jnp.float32),
    )
    carried = initial
    start_row = jnp.int32(0)
    piece_keys = lax.all_gather(merged_keys, "ctx", axis=0, tiled=True)
    piece_values = lax.all_gather(merged_values, "ctx", axis=0, tiled=True)
    piece_rows = piece_keys.shape[0]
    block_rows = min(512, piece_rows)
    for lower in range(0, piece_rows, block_rows):
        upper = min(lower + block_rows, piece_rows)
        block_keys = piece_keys[lower:upper].reshape(upper - lower, groups, HD)
        block_values = piece_values[lower:upper].reshape(upper - lower, groups, HD)
        key_place = start_row + lower + jnp.arange(upper - lower, dtype=jnp.int32)

        def update(state_in):
            return attend_block(
                state_in, query_split, query_place, block_keys, block_values, key_place, score_scale
            )

        carried = lax.cond(
            start_row + lower <= first_row + token_count - 1, update, unchanged, carried
        )
    running_max, denominator, numerator = carried
    attention = (
        (numerator / denominator[..., None])
        .reshape(token_count, head_count * HD)
        .astype(jnp.bfloat16)
    )
    partial_value = jnp.dot(attention, value_head, preferred_element_type=jnp.float32)
    value_out = lax.psum(partial_value, "tp")
    return (attention[None], value_out[None])


def solution(mesh):
    in_specs = (
        P("dp", "ctx", "tp"),
        P("dp", "ctx", "tp"),
        P("dp", "ctx", "tp"),
        P("dp", "ctx", None, None, "tp"),
        P("dp", "ctx", None, None),
        P("dp", "ctx", None),
        P("tp"),
    )
    out_specs = (P("dp", "ctx", "tp"), P("dp", "ctx"))
    return jax.shard_map(body, mesh=mesh, in_specs=in_specs, out_specs=out_specs, check_vma=False)
```

profile of v0, /device:TPU:0, one launch (start us, length us, event | category | flops | bytes accessed | tf_op | source)
XLA Modules:
  0.0 53.5 jit_solution(15466480431015100622)
XLA Ops:
  0.6 0.7 %fusion.25 = s32[8,4]{0,1:T(4,128)S(1)} fusion(s32[8]{0:T(128)} %bitcast.58), kind=kLoop, calls=%fused_computation.37 | loop fusion | flops 64 | bytes 160 | tf_op jit(solution)/shard_map/convert_element_type | solution.py:48
  1.3 0.2 reduce_window_sum.11
  1.5 0.7 %select_reduce_fusion.1 = s32[8]{0:T(128)S(1)} fusion(s32[8,4]{0,1:T(4,128)S(1)} %reduce_window_sum.11, s32[8]{0:T(128)} %bitcast.59), kind=kLoop, calls=%fused_computation.35 | loop fusion | flops 152 | bytes 192 | tf_op jit(solution)/shard_map/reduce_sum | solution.py:52
  2.2 0.7 %multiply_add_fusion.1 = s32[8]{0:T(128)S(1)} fusion(s32[8]{0:T(128)S(1)} %select_reduce_fusion.1, s32[1,1,8,1]{2,3,1,0:T(1,128)} %param.13), kind=kLoop, calls=%fused_computation.39 | loop fusion | flops 16 | bytes 96 | tf_op jit(solution)/shard_map/add | solution.py:53
  2.8 0.7 %convert_reduce_fusion = (s32[16]{0:T(128)S(1)}, s32[16]{0:T(128)S(1)}) fusion(s32[8]{0:T(128)S(1)} %multiply_add_fusion.1, s32[8]{0:T(128)} %bitcast.60), kind=kLoop, calls=%fused_computation.31 | loop fusion | flops 608 | bytes 192 | tf_op jit(solution)/shard_map/reduce_sum | solution.py:59
  3.6 0.7 %add.48 = s32[4,4,1]{1,0,2:T(4,128)} reshape(s32[16]{0:T(128)S(1)} %multiply_add_fusion) | data formatting | bytes 128 | tf_op jit(solution)/shard_map/add | solution.py:60
  4.2 6.3 %all-to-all-start = ((s32[4,4,1]{1,2,0:T(1,128)}), s32[4,4,1]{1,2,0:T(1,128)S(1)}, u32[]{:S(2)}, u32[]{:S(2)}) async-start(s32[4,4,1]{1,2,0:T(1,128)} %bitcast.7), calls=%async_computation | async-start | bytes 4096 | tf_op jit(solution)/shard_map/all_to_all | solution.py:64
  10.6 0.7 %copy.45 = bf16[1,8,2,256]{3,1,2,0:T(8,128)(2,1)S(1)} copy(bf16[1,8,2,256]{3,2,1,0:T(2,128)(2,1)} %bitcast.56) | data formatting | bytes 16384
  11.3 0.3 convolution_convert_fusion
  11.5 0.6 %reshape.108 = bf16[16,2,256]{2,1,0:T(2,128)(2,1)} reshape(bf16[16,512]{1,0:T(8,128)(2,1)S(1)} %convolution_convert_fusion) | data formatting | bytes 32768 | tf_op jit(solution)/shard_map/reshape | solution.py:61
  12.2 3.8 %all-to-all-done = s32[4,4,1]{1,2,0:T(1,128)S(1)} async-done(((s32[4,4,1]{1,2,0:T(1,128)}), s32[4,4,1]{1,2,0:T(1,128)S(1)}, u32[]{:S(2)}, u32[]{:S(2)}) %all-to-all-start) | async-done | bytes 96 | tf_op jit(solution)/shard_map/all_to_all | solution.py:64
  16.0 3.3 %all-to-all-start.1 = ((bf16[16,2,256]{2,1,0:T(2,128)(2,1)}), bf16[16,2,256]{2,1,0:T(2,128)(2,1)S(1)}, u32[]{:S(2)}, u32[]{:S(2)}) async-start(bf16[16,2,256]{2,1,0:T(2,128)(2,1)} %reshape.108), calls=%async_computation.1 | async-start | bytes 32768 | tf_op jit(solution)/shard_map/all_to_all | solution.py:63
  19.3 0.7 %reshape.114 = bf16[2048,1]{0,1:T(2,128)(2,1)S(1)} reshape(bf16[2048]{0:T(1024)(128)(2,1)} %param.15) | data formatting | bytes 8192 | tf_op args[6]
  20.0 0.6 %broadcast.91 = s32[]{:T(128)} broadcast(s32[]{:T(128)} %constant.11.clone.1), dimensions={} | broadcast | bytes 8 | tf_op jit(solution)/shard_map/all_to_all | solution.py:64
  20.6 0.7 %reduce.3 = s32[4,4]{1,0:T(4,128)S(1)} reduce(s32[4,4,1]{1,2,0:T(1,128)S(1)} %all-to-all-done, s32[]{:T(128)} %broadcast.91), dimensions={2}, to_apply=%all_to_all.7.reduce_sub_computation.3 | reduce | bytes 132 | tf_op jit(solution)/shard_map/all_to_all | solution.py:64
  21.4 3.5 %all-to-all-done.1 = bf16[16,2,256]{2,1,0:T(2,128)(2,1)S(1)} async-done(((bf16[16,2,256]{2,1,0:T(2,128)(2,1)}), bf16[16,2,256]{2,1,0:T(2,128)(2,1)S(1)}, u32[]{:S(2)}, u32[]{:S(2)}) %all-to-all-start.1) | async-done | bytes 16416 | tf_op jit(solution)/shard_map/all_to_all | solution.py:63
  24.9 0.2 fusion.22
  25.0 0.9 %fusion.20 = (bf16[128,256]{1,0:T(8,128)(2,1)S(1)}, bf16[128,256]{1,0:T(8,128)(2,1)S(1)}) fusion(f32[128,512]{1,0:T(8,128)S(1)} %fusion.22, bf16[1,128,256]{2,1,0:T(8,128)(2,1)} %param.11, bf16[1,128,256]{2,1,0:T(8,128)(2,1)} %param.10), kind=kLoop, calls=%fused_computation.24 | loop fusion | flops 196608 | bytes 524288 | tf_op jit(solution)/shard_map/convert_element_type | solution.py:73
  25.9 5.8 %all_gather.6 = bf16[512,256]{1,0:T(8,128)(2,1)S(1)} all-gather(bf16[128,256]{1,0:T(8,128)(2,1)S(1)} %get-tuple-element.45), channel_id=1, replica_groups=mesh['dp'=4,'ctx'=4,'tp'=2] {'ctx'}, dimensions={0}, use_global_device_ids=true | all-gather | bytes 327680 | tf_op jit(solution)/shard_map/all_gather | solution.py:86
  31.7 5.8 %all_gather.7 = bf16[512,256]{1,0:T(8,128)(2,1)S(1)} all-gather(bf16[128,256]{1,0:T(8,128)(2,1)S(1)} %get-tuple-element.44), channel_id=1, replica_groups=mesh['dp'=4,'ctx'=4,'tp'=2] {'ctx'}, dimensions={0}, use_global_device_ids=true | all-gather | bytes 327680 | tf_op jit(solution)/shard_map/all_gather | solution.py:87
  37.6 9.2 %conditional.1 = (f32[128,2,8]{0,2,1:T(8,128)S(1)}, f32[128,2,8,128]{0,3,2,1:T(8,128)S(1)}) conditional(s32[]{:T(128)} %convert_element_type.53, () %tuple.16, (s32[512]{0:T(512)S(1)}, s32[]{:T(128)}, s32[128]{0:T(128)S(1)}, bf16[512,256]{1,0:T(8,128)(2,1)S(1)}, bf16[1,128,2048]{2,1,0:T(8,128)(2,1)}, /*index=5*/bf16[512,256]{1,0:T(8,128)(2,1)S(1)}) %tuple.17), branch_computations={%region_4.5_spmd, %region_5.8_spmd} | conditional | flops 550836352 | bytes 36007472 | solution.py:101
  37.6 0.1 broadcast_compare_fusion
  37.7 1.1 %copy.44 = bf16[16,8,16,128]{3,2,1,0:T(8,128)(2,1)S(1)} copy(bf16[16,8,16,128]{3,1,2,0:T(8,128)(2,1)} %bitcast.52) | data formatting | bytes 1048576 | tf_op jit(solution)/shard_map/cond
  38.9 0.8 %fusion = (f32[128,2,8]{0,2,1:T(8,128)S(1)}, f32[2,512,128,8]{2,1,3,0:T(8,128)S(1)}) fusion(pred[128,512]{0,1:T(8,128)(4,1)S(1)} %broadcast_compare_fusion, bf16[128,2,8,128]{3,2,1,0:T(8,128)(2,1)S(1)} %bitcast.50, bf16[512,2,128,1]{2,1,0,3:T(2,128)(2,1)S(1)} %bitcast.51), kind=kOutput, calls=%fused_computation.2 | convolution fusion | flops 271579136 | bytes 5054464 | tf_op jit(solution)/shard_map/cond/branch_1_fun/tgrd,sgd->tgrs/dot_general | solution.py:15
  39.7 1.9 %copy-done = f32[2,512,128,8]{2,1,3,0:T(8,128)} copy-done((f32[2,512,128,8]{2,1,3,0:T(8,128)}, f32[2,512,128,8]{2,1,3,0:T(8,128)S(1)}, u32[]{:S(2)}) %copy-start) | copy-done | bytes 4194328 | tf_op jit(solution)/shard_map/cond
  41.7 1.0 %fusion.2 = f32[128,2,8]{0,2,1:T(8,128)S(1)} fusion(f32[2,512,128,8]{2,1,3,0:T(8,128)S(1)} %get-tuple-element.43, f32[128,2,8]{0,2,1:T(8,128)S(1)} %broadcast_maximum_fusion, pred[128,512]{0,1:T(8,128)(4,1)S(1)} %broadcast_compare_fusion), kind=kLoop, calls=%fused_computation.4 | loop fusion | flops 5240832 | bytes 4276224 | tf_op jit(solution)/shard_map/cond/branch_1_fun/reduce_sum | solution.py:23
  42.8 3.7 %fusion.9 = f32[128,2,8,128]{3,0,2,1:T(8,128)S(1)} fusion(f32[2,512,128,8]{2,1,3,0:T(8,128)} %copy-done, f32[128,2,8]{0,2,1:T(8,128)S(1)} %broadcast_maximum_fusion, pred[128,512]{0,1:T(8,128)(4,1)S(1)} %broadcast_compare_fusion, f32[128,2,8]{0,2,1:T(8,128)S(1)} %get-tuple-element.40, bf16[512,2,128,1]{2,1,0,3:T(2,128)(2,1)S(1)} %bitcast.53), kind=kOutput, calls=%fused_computation.8 | convolution fusion | flops 273940480 | bytes 5586944 | tf_op jit(solution)/shard_map/cond/branch_1_fun/tgrs,sgd->tgrd/dot_general | solution.py:24
  46.5 0.3 copy.43
  46.8 0.1 divide_convert_fusion
  46.9 1.0 %copy.34 = bf16[1,128,2048]{2,1,0:T(8,128)(2,1)} copy(bf16[1,128,2048]{1,2,0:T(8,128)(2,1)S(1)} %bitcast.48) | data formatting | bytes 1048576
  47.9 0.2 fusion.26
  48.1 5.4 %psum.7 = f32[1,128]{1,0:T(1,128)} all-reduce(f32[1,128]{1,0:T(1,128)S(1)} %fusion.26), channel_id=1, replica_groups=mesh['dp'=4,'ctx'=4,'tp'=2] {'tp'}, use_global_device_ids=true, to_apply=%region_8.9 | all-reduce | flops 128 | bytes 1024 | tf_op jit(solution)/shard_map/psum | solution.py:111
  (11 shorter events, 0.3 us)
Async XLA Ops:
  4.2 11.8 %all-to-all-start = ((s32[4,4,1]{1,2,0:T(1,128)}), s32[4,4,1]{1,2,0:T(1,128)S(1)}, u32[]{:S(2)}, u32[]{:S(2)}) async-start(s32[4,4,1]{1,2,0:T(1,128)} %bitcast.7), calls=%async_computation | async-start | bytes 4096 | tf_op jit(solution)/shard_map/all_to_all | solution.py:64
  16.0 8.8 %all-to-all-start.1 = ((bf16[16,2,256]{2,1,0:T(2,128)(2,1)}), bf16[16,2,256]{2,1,0:T(2,128)(2,1)S(1)}, u32[]{:S(2)}, u32[]{:S(2)}) async-start(bf16[16,2,256]{2,1,0:T(2,128)(2,1)} %reshape.108), calls=%async_computation.1 | async-start | bytes 32768 | tf_op jit(solution)/shard_map/all_to_all | solution.py:63
  39.7 1.9 %copy-start = (f32[2,512,128,8]{2,1,3,0:T(8,128)}, f32[2,512,128,8]{2,1,3,0:T(8,128)S(1)}, u32[]{:S(2)}) copy-start(f32[2,512,128,8]{2,1,3,0:T(8,128)S(1)} %get-tuple-element.43) | copy-start | bytes 12582916 | tf_op jit(solution)/shard_map/cond
where the time goes:
time: 54.1 us; the launch traced here: 53.5 us
  blocking collectives  17 us (31%)
  starting transfers between devices  9.6 us (18%)
  local copies, waits for them, and re-layouts  7.91 us (15%)
  waiting for transfers between devices  7.34 us (14%)
  other arithmetic  5.85 us (11%)
  matrix products  5.05 us (9%)
  between operations  0.68 us (1%)
    all_to_all x1, starting transfers between devices, body(): lax.all_to_all(slot_place, 'dp', split_axis=0, concat_axis=0, tiled=True)  6.35 us
    all_gather x1, blocking collectives, body(): piece_values = lax.all_gather(merged_values, 'ctx', axis=0, tiled=True)  5.84 us
    all_gather x1, blocking collectives, body(): piece_keys = lax.all_gather(merged_keys, 'ctx', axis=0, tiled=True)  5.78 us
    psum x1, blocking collectives, body(): value_out = lax.psum(partial_value, 'tp')  5.42 us
    all_to_all x1, waiting for transfers between devices, body(): lax.all_to_all(slot_place, 'dp', split_axis=0, concat_axis=0, tiled=True)  3.85 us
    dot_general x1, matrix products, attend_block(): jnp.einsum('tgrs,sgd->tgrd', weights.astype(jnp.bfloat16), block_values,...  3.67 us
    all_to_all x1, waiting for transfers between devices, body(): lax.all_to_all(packed, 'dp', split_axis=0, concat_axis=0, tiled=True)  3.49 us
    all_to_all x1, starting transfers between devices, body(): lax.all_to_all(packed, 'dp', split_axis=0, concat_axis=0, tiled=True)  3.25 us
  transfers between devices with their start and end apart: 2, of which 2 were waited for; matrix products, arithmetic and copies ran while one was open for 7% of the time, Pallas kernels for 0%

commit v1 on v0

--- a/solution.py
+++ b/solution.py
@@ -83,8 +83,13 @@
     )
     carried = initial
     start_row = jnp.int32(0)
-    piece_keys = lax.all_gather(merged_keys, "ctx", axis=0, tiled=True)
-    piece_values = lax.all_gather(merged_values, "ctx", axis=0, tiled=True)
+    piece_keys, piece_values = jnp.split(
+        lax.all_gather(
+            jnp.concatenate([merged_keys, merged_values], axis=1), "ctx", axis=0, tiled=True
+        ),
+        [merged_keys.shape[1]],
+        axis=1,
+    )
     piece_rows = piece_keys.shape[0]
     block_rows = min(512, piece_rows)
     for lower in range(0, piece_rows, block_rows):

time: 54.1 us -> 45.7 us (0.84)
  blocking collectives: 17 us -> 12.6 us
  matrix products: 5.05 us -> 2.94 us
  local copies, waits for them, and re-layouts: 7.91 us -> 6.03 us
    all_gather x2 -> x1, blocking collectives: 11.6 us -> 7.2 us  [body(): lax.all_gather(jnp.concatenate([merged_keys, merged_values], axis=1), 'ct...]
    dot_general x1, matrix products: 3.67 us -> 1.47 us  [attend_block(): jnp.einsum('tgrs,sgd->tgrd', weights.astype(jnp.bfloat16), block_values,...]
    cond x3 -> x1, local copies, waits for them, and re-layouts: 3.05 us -> 1.15 us
  transfers between devices with their start and end apart: 2 -> 2, of which waited for: 2 -> 2; matrix products, arithmetic and copies ran while one was open for 7% -> 8% of each run, Pallas kernels for 0% -> 0%
where the time goes in v1:
time: 45.7 us; the launch traced here: 45.2 us
  blocking collectives  12.6 us (28%)
  starting transfers between devices  9.6 us (21%)
  waiting for transfers between devices  7.56 us (17%)
  local copies, waits for them, and re-layouts  6.03 us (13%)
  other arithmetic  5.7 us (12%)
  matrix products  2.94 us (6%)
  between operations  0.69 us (2%)
    all_gather x1, blocking collectives, body(): lax.all_gather(jnp.concatenate([merged_keys, merged_values], axis=1), 'ct...  7.2 us
    all_to_all x1, starting transfers between devices, body(): lax.all_to_all(slot_place, 'dp', split_axis=0, concat_axis=0, tiled=True)  6.35 us
    psum x1, blocking collectives, body(): value_out = lax.psum(partial_value, 'tp')  5.42 us
    all_to_all x1, waiting for transfers between devices, body(): lax.all_to_all(slot_place, 'dp', split_axis=0, concat_axis=0, tiled=True)  3.85 us
    all_to_all x1, waiting for transfers between devices, body(): lax.all_to_all(packed, 'dp', split_axis=0, concat_axis=0, tiled=True)  3.71 us
    all_to_all x1, starting transfers between devices, body(): lax.all_to_all(packed, 'dp', split_axis=0, concat_axis=0, tiled=True)  3.25 us
    unnamed x4, local copies, waits for them, and re-layouts  2.41 us
    dot_general x1, matrix products, attend_block(): jnp.einsum('tgrs,sgd->tgrd', weights.astype(jnp.bfloat16), block_values,...  1.47 us
  transfers between devices with their start and end apart: 2, of which 2 were waited for; matrix products, arithmetic and copies ran while one was open for 8% of the time, Pallas kernels for 0%

profile of v1, /device:TPU:0, one launch (start us, length us, event | category | flops | bytes accessed | tf_op | source)
XLA Modules:
  0.0 45.2 jit_solution(2996413573991728077)
XLA Ops:
  0.6 0.7 %fusion.23 = s32[8,4]{0,1:T(4,128)S(1)} fusion(s32[8]{0:T(128)} %bitcast.68), kind=kLoop, calls=%fused_computation.36 | loop fusion | flops 64 | bytes 160 | tf_op jit(solution)/shard_map/convert_element_type | solution.py:48
  1.3 0.2 reduce_window_sum.11
  1.5 0.7 %select_reduce_fusion.1 = s32[8]{0:T(128)S(1)} fusion(s32[8,4]{0,1:T(4,128)S(1)} %reduce_window_sum.11, s32[8]{0:T(128)} %bitcast.69), kind=kLoop, calls=%fused_computation.34 | loop fusion | flops 152 | bytes 192 | tf_op jit(solution)/shard_map/reduce_sum | solution.py:52
  2.2 0.7 %multiply_add_fusion.1 = s32[8]{0:T(128)S(1)} fusion(s32[8]{0:T(128)S(1)} %select_reduce_fusion.1, s32[1,1,8,1]{2,3,1,0:T(1,128)} %param.13), kind=kLoop, calls=%fused_computation.38 | loop fusion | flops 16 | bytes 96 | tf_op jit(solution)/shard_map/add | solution.py:53
  2.8 0.7 %convert_reduce_fusion = (s32[16]{0:T(128)S(1)}, s32[16]{0:T(128)S(1)}) fusion(s32[8]{0:T(128)S(1)} %multiply_add_fusion.1, s32[8]{0:T(128)} %bitcast.70), kind=kLoop, calls=%fused_computation.30 | loop fusion | flops 608 | bytes 192 | tf_op jit(solution)/shard_map/reduce_sum | solution.py:59
  3.6 0.7 %add.48 = s32[4,4,1]{1,0,2:T(4,128)} reshape(s32[16]{0:T(128)S(1)} %multiply_add_fusion) | data formatting | bytes 128 | tf_op jit(solution)/shard_map/add | solution.py:60
  4.2 6.3 %all-to-all-start = ((s32[4,4,1]{1,2,0:T(1,128)}), s32[4,4,1]{1,2,0:T(1,128)S(1)}, u32[]{:S(2)}, u32[]{:S(2)}) async-start(s32[4,4,1]{1,2,0:T(1,128)} %bitcast.9), calls=%async_computation | async-start | bytes 4096 | tf_op jit(solution)/shard_map/all_to_all | solution.py:64
  10.6 0.7 %copy.46 = bf16[1,8,2,256]{3,1,2,0:T(8,128)(2,1)S(1)} copy(bf16[1,8,2,256]{3,2,1,0:T(2,128)(2,1)} %bitcast.66) | data formatting | bytes 16384
  11.3 0.3 convolution_convert_fusion
  11.5 0.6 %reshape.108 = bf16[16,2,256]{2,1,0:T(2,128)(2,1)} reshape(bf16[16,512]{1,0:T(8,128)(2,1)S(1)} %convolution_convert_fusion) | data formatting | bytes 32768 | tf_op jit(solution)/shard_map/reshape | solution.py:61
  12.2 3.8 %all-to-all-done = s32[4,4,1]{1,2,0:T(1,128)S(1)} async-done(((s32[4,4,1]{1,2,0:T(1,128)}), s32[4,4,1]{1,2,0:T(1,128)S(1)}, u32[]{:S(2)}, u32[]{:S(2)}) %all-to-all-start) | async-done | bytes 96 | tf_op jit(solution)/shard_map/all_to_all | solution.py:64
  16.0 3.3 %all-to-all-start.1 = ((bf16[16,2,256]{2,1,0:T(2,128)(2,1)}), bf16[16,2,256]{2,1,0:T(2,128)(2,1)S(1)}, u32[]{:S(2)}, u32[]{:S(2)}) async-start(bf16[16,2,256]{2,1,0:T(2,128)(2,1)} %reshape.108), calls=%async_computation.1 | async-start | bytes 32768 | tf_op jit(solution)/shard_map/all_to_all | solution.py:63
  19.3 0.7 %reshape.114 = bf16[2048,1]{0,1:T(2,128)(2,1)S(1)} reshape(bf16[2048]{0:T(1024)(128)(2,1)} %param.15) | data formatting | bytes 8192 | tf_op args[6]
  20.0 0.5 %broadcast.91 = s32[]{:T(128)} broadcast(s32[]{:T(128)} %constant.11.clone.1), dimensions={} | broadcast | bytes 8 | tf_op jit(solution)/shard_map/all_to_all | solution.py:64
  20.5 0.6 %reduce.3 = s32[4,4]{1,0:T(4,128)S(1)} reduce(s32[4,4,1]{1,2,0:T(1,128)S(1)} %all-to-all-done, s32[]{:T(128)} %broadcast.91), dimensions={2}, to_apply=%all_to_all.7.reduce_sub_computation.3 | reduce | bytes 132 | tf_op jit(solution)/shard_map/all_to_all | solution.py:64
  21.1 0.1 eq.48
  21.1 3.7 %all-to-all-done.1 = bf16[16,2,256]{2,1,0:T(2,128)(2,1)S(1)} async-done(((bf16[16,2,256]{2,1,0:T(2,128)(2,1)}), bf16[16,2,256]{2,1,0:T(2,128)(2,1)S(1)}, u32[]{:S(2)}, u32[]{:S(2)}) %all-to-all-start.1) | async-done | bytes 16416 | tf_op jit(solution)/shard_map/all_to_all | solution.py:63
  24.9 0.2 fusion.20
  25.0 0.9 %fusion.19 = (bf16[128,256]{1,0:T(8,128)(2,1)S(1)}, bf16[128,256]{1,0:T(8,128)(2,1)S(1)}) fusion(f32[128,512]{1,0:T(8,128)S(1)} %fusion.20, bf16[1,128,256]{2,1,0:T(8,128)(2,1)} %param.10, bf16[1,128,256]{2,1,0:T(8,128)(2,1)} %param.11), kind=kLoop, calls=%fused_computation.24 | loop fusion | flops 196608 | bytes 524288 | tf_op jit(solution)/shard_map/convert_element_type | solution.py:72
  25.9 7.2 %all_gather.3 = bf16[512,512]{1,0:T(8,128)(2,1)S(1)} all-gather(bf16[128,512]{1,0:T(8,128)(2,1)S(1)} %pad_maximum_fusion), channel_id=1, replica_groups=mesh['dp'=4,'ctx'=4,'tp'=2] {'ctx'}, dimensions={0}, use_global_device_ids=true | all-gather | bytes 655360 | tf_op jit(solution)/shard_map/all_gather | solution.py:87
  33.2 5.3 %conditional.1 = (f32[128,2,8]{0,2,1:T(8,128)S(1)}, f32[128,2,8,128]{0,3,2,1:T(8,128)S(1)}) conditional(s32[]{:T(128)} %convert_element_type.53, () %tuple.16, (s32[512]{0:T(512)S(1)}, s32[]{:T(128)}, s32[128]{0:T(128)S(1)}, bf16[512,512]{1,0:T(8,128)(2,1)S(1)}, bf16[1,128,2048]{2,1,0:T(8,128)(2,1)}) %tuple.17), branch_computations={%region_4.5_spmd, %region_5.8_spmd} | conditional | flops 550836352 | bytes 20278804 | solution.py:106
  33.2 0.1 broadcast_compare_fusion
  33.3 0.2 copy.33
  33.6 1.1 %copy.45 = bf16[16,8,16,128]{3,2,1,0:T(8,128)(2,1)S(1)} copy(bf16[16,8,16,128]{3,1,2,0:T(8,128)(2,1)} %bitcast.62) | data formatting | bytes 1048576 | tf_op jit(solution)/shard_map/cond
  34.7 0.9 %fusion = (f32[128,2,8]{0,2,1:T(8,128)S(1)}, f32[2,512,128,8]{2,1,3,0:T(8,128)S(1)}) fusion(pred[128,512]{0,1:T(8,128)(4,1)S(1)} %broadcast_compare_fusion, bf16[512,2,128,1]{0,2,3,1:T(8,128)(2,1)S(1)} %bitcast.61, bf16[128,2,8,128]{3,2,1,0:T(8,128)(2,1)S(1)} %bitcast.60), kind=kOutput, calls=%fused_computation.2 | convolution fusion | flops 271579136 | bytes 5054464 | tf_op jit(solution)/shard_map/cond/branch_1_fun/tgrd,sgd->tgrs/dot_general | solution.py:15
  35.6 1.0 %fusion.2 = f32[128,2,8]{0,2,1:T(8,128)S(1)} fusion(f32[2,512,128,8]{2,1,3,0:T(8,128)S(1)} %get-tuple-element.60, f32[128,2,8]{0,2,1:T(8,128)S(1)} %broadcast_maximum_fusion, pred[128,512]{0,1:T(8,128)(4,1)S(1)} %broadcast_compare_fusion), kind=kLoop, calls=%fused_computation.4 | loop fusion | flops 5240832 | bytes 4276224 | tf_op jit(solution)/shard_map/cond/branch_1_fun/reduce_sum | solution.py:23
  36.6 1.5 %fusion.9 = f32[128,2,8,128]{3,0,2,1:T(8,128)S(1)} fusion(bf16[512,2,128,1]{0,2,3,1:T(8,128)(2,1)S(1)} %bitcast.63, f32[2,512,128,8]{2,1,3,0:T(8,128)S(1)} %get-tuple-element.60, f32[128,2,8]{0,2,1:T(8,128)S(1)} %broadcast_maximum_fusion, pred[128,512]{0,1:T(8,128)(4,1)S(1)} %broadcast_compare_fusion, f32[128,2,8]{0,2,1:T(8,128)S(1)} %get-tuple-element.57), kind=kOutput, calls=%fused_computation.8 | convolution fusion | flops 273940480 | bytes 5586944 | tf_op jit(solution)/shard_map/cond/branch_1_fun/tgrs,sgd->tgrd/dot_general | solution.py:24
  38.1 0.3 copy.44
  38.5 0.1 divide_convert_fusion
  38.6 1.0 %copy.35 = bf16[1,128,2048]{2,1,0:T(8,128)(2,1)} copy(bf16[1,128,2048]{1,2,0:T(8,128)(2,1)S(1)} %bitcast.58) | data formatting | bytes 1048576
  39.6 0.2 fusion.25
  39.8 5.4 %psum.7 = f32[1,128]{1,0:T(1,128)} all-reduce(f32[1,128]{1,0:T(1,128)S(1)} %fusion.25), channel_id=1, replica_groups=mesh['dp'=4,'ctx'=4,'tp'=2] {'tp'}, use_global_device_ids=true, to_apply=%region_8.9 | all-reduce | flops 128 | bytes 1024 | tf_op jit(solution)/shard_map/psum | solution.py:116
  (9 shorter events, 0.1 us)
Async XLA Ops:
  4.2 11.8 %all-to-all-start = ((s32[4,4,1]{1,2,0:T(1,128)}), s32[4,4,1]{1,2,0:T(1,128)S(1)}, u32[]{:S(2)}, u32[]{:S(2)}) async-start(s32[4,4,1]{1,2,0:T(1,128)} %bitcast.9), calls=%async_computation | async-start | bytes 4096 | tf_op jit(solution)/shard_map/all_to_all | solution.py:64
  16.0 8.8 %all-to-all-start.1 = ((bf16[16,2,256]{2,1,0:T(2,128)(2,1)}), bf16[16,2,256]{2,1,0:T(2,128)(2,1)S(1)}, u32[]{:S(2)}, u32[]{:S(2)}) async-start(bf16[16,2,256]{2,1,0:T(2,128)(2,1)} %reshape.108), calls=%async_computation.1 | async-start | bytes 32768 | tf_op jit(solution)/shard_map/all_to_all | solution.py:63
